TPU v7x, 32 devices: a whole 2x2x4 slice. The times are simulated.
32 devices in a mesh: sp: 2 (over core), py: 4 (over z), pz: 4 (over y, x).
Axes of the slice: x: 2, y: 2, z: 4, core: 2. Of those that a mesh axis runs over, the one named last changes fastest.
Arguments:
- concentration: float32 [8, 128, 128, 128], P('sp', 'py', 'pz'), may hold values from -1 to 1.1
- mobility: float32 [8, 8], replicated, may hold values from 0.1 to 0.6
- kappa: float32 [8], replicated, may hold values from 0.5 to 2
- well_depth: float32 [8], P('sp'), may hold values from 0.5 to 2
Outputs:
- updated: float32 [8, 128, 128, 128], P('sp', 'py', 'pz')
All inputs are finite; a program needn't handle non-finite values.
Results may differ from a plain program's by a relative error of at most 0.000084.
Values sent between devices are 32-bit elements; how exact they have to be, the bound alone decides.
A program may use at most 128 MiB of HBM per device.

v0:
```python
import math
import jax
import jax.numpy as jnp
from jax import lax
from jax.sharding import PartitionSpec as P


def tables(count):
    modes = jnp.arange(count, dtype=jnp.int32)
    product = modes[:, None] * modes[None, :] % count
    angle = 2.0 * math.pi * product.astype(jnp.float32) / count
    return (jnp.cos(angle), jnp.sin(angle))


def wave_square(index, count):
    freq = jnp.where(index < count // 2, index, index - count).astype(jnp.float32)
    return (2.0 * math.pi * freq / count) ** 2


def contract(form, values, table):
    return jnp.einsum(form, values, table, precision=lax.Precision.HIGHEST)


def rotate(spectrum, form, count, forward):
    cosine, sine = tables(count)
    real_part, imag_part = (spectrum[0], spectrum[1])
    real_cos = contract(form, real_part, cosine)
    real_sin = contract(form, real_part, sine)
    imag_cos = contract(form, imag_part, cosine)
    imag_sin = contract(form, imag_part, sine)
    if forward:
        return jnp.stack([real_cos + imag_sin, imag_cos - real_sin])
    return jnp.stack([real_cos - imag_sin, imag_cos + real_sin])


def per_device(concentration, mobility, kappa, well_depth):
    local_species, rows_x, rows_y, depth = concentration.shape
    count_sp = lax.axis_size("sp")
    count_py = lax.axis_size("py")
    count_pz = lax.axis_size("pz")
    full_x = rows_x * count_py
    full_y = rows_y * count_pz
    half_depth = depth // 2
    bulk = well_depth[:, None, None, None] * (
        concentration * concentration * concentration - concentration
    )
    fields = jnp.stack([concentration, bulk])
    cosine, sine = tables(depth)
    alternate = (1 - 2 * (jnp.arange(depth, dtype=jnp.int32) % 2)).astype(jnp.float32)
    spectrum = jnp.stack(
        [
            contract("fsxyz,zk->fsxyk", fields, cosine[:, :half_depth]),
            -contract("fsxyz,zk->fsxyk", fields, sine[:, :half_depth]),
        ]
    )
    spectrum = lax.all_to_all(spectrum, "pz", split_axis=5, concat_axis=4, tiled=True)
    own_lines = spectrum.shape[5]
    highest = contract("fsxyz,z->fsxy", fields, alternate)
    highest = lax.all_gather(highest, "pz", axis=3, tiled=True)
    highest = jnp.stack([highest, jnp.zeros_like(highest)])[..., None]
    spectrum = jnp.concatenate([spectrum, highest], axis=5)
    z_modes = jnp.concatenate(
        [
            lax.axis_index("pz") * own_lines + jnp.arange(own_lines, dtype=jnp.int32),
            jnp.full((1,), half_depth, jnp.int32),
        ]
    )
    spectrum = rotate(spectrum, "fsxyz,yk->fsxkz", full_y, True)
    spectrum = lax.all_to_all(
        lax.all_to_all(spectrum, "sp", split_axis=4, concat_axis=2, tiled=True),
        "py",
        split_axis=4,
        concat_axis=3,
        tiled=True,
    )
    spectrum = rotate(spectrum, "fsxyz,xk->fskyz", full_x, True)
    narrow = spectrum.shape[4]
    lines = spectrum.shape[5]
    y_start = (lax.axis_index("sp") * count_py + lax.axis_index("py")) * narrow
    ksq_x = wave_square(jnp.arange(full_x, dtype=jnp.int32), full_x)
    ksq_y = wave_square(y_start + jnp.arange(narrow, dtype=jnp.int32), full_y)
    ksq_z = wave_square(z_modes, depth)
    ksq = ksq_x[:, None, None] + ksq_y[None, :, None] + ksq_z[None, None, :]
    c_hat = spectrum[:, 0]
    drive = spectrum[:, 1] + kappa[None, :, None, None, None] * ksq[None, None] * c_hat
    mix = jnp.einsum("ij,rjxyz->rixyz", mobility, drive, precision=lax.Precision.HIGHEST)
    stiff = 0.5 * (jnp.diagonal(mobility) * kappa)[:, None, None, None] * (ksq * ksq)[None]
    new_hat = (c_hat * (1.0 + stiff)[None] - 0.5 * ksq[None, None] * mix) / (1.0 + stiff)[None]
    new_hat = rotate(new_hat, "sxyz,xk->skyz", full_x, False)
    moved = lax.all_to_all(
        lax.all_to_all(new_hat, "sp", split_axis=1, concat_axis=3, tiled=True),
        "py",
        split_axis=2,
        concat_axis=3,
        tiled=True,
    )
    moved = moved.reshape(2, local_species, rows_x, count_py, count_sp, narrow, lines)
    moved = moved.transpose(0, 1, 2, 4, 3, 5, 6).reshape(2, local_species, rows_x, full_y, lines)
    moved = rotate(moved, "sxyz,yk->sxkz", full_y, False)
    main = moved[..., : lines - 1]
    highest = moved[0, :, :, :, lines - 1]
    main = lax.all_to_all(main, "pz", split_axis=3, concat_axis=4, tiled=True)
    highest = lax.dynamic_slice_in_dim(highest, lax.axis_index("pz") * rows_y, rows_y, 2)
    weight = jnp.where(jnp.arange(half_depth, dtype=jnp.int32) == 0, 1.0, 2.0).astype(jnp.float32)
    result = contract("sxyk,kz->sxyz", main[0] * weight, cosine[:half_depth]) - contract(
        "sxyk,kz->sxyz", main[1] * weight, sine[:half_depth]
    )
    result = result + highest[..., None] * alternate[None, None, None, :]
    return result * (1.0 / (full_x * full_y * depth))


def solution(mesh):
    in_specs = (P("sp", "py", "pz", None), P(), P(), P("sp"))
    out_specs = P("sp", "py", "pz", None)
    return jax.shard_map(
        per_device, mesh=mesh, in_specs=in_specs, out_specs=out_specs, check_vma=False
    )
```

profile of v0, /device:TPU:0, one launch (start us, length us, event | category | flops | bytes accessed | tf_op | source)
XLA Modules:
  0.0 783.9 jit_solution(356317510580128092)
XLA Ops:
  0.5 2.2 fusion.19
  2.7 3.4 fusion.17
  6.2 3.4 negate_bitcast_fusion
  9.6 4.3 pad_maximum_fusion
  13.9 16.6 %copy.169 = f32[2,2,4,32,32,64]{4,3,2,1,0,5:T(8,128)} copy(f32[2,2,4,32,32,64]{5,4,3,2,1,0:T(8,128)} %pad_maximum_fusion) | data formatting | bytes 8388608 | tf_op jit(solution)/shard_map/stack | solution.py:50
  30.5 11.5 %reshape.175 = f32[4,1,262144]{2,1,0:T(1,128)} reshape(f32[64,2,2,4,32,32]{5,4,3,2,1,0:T(8,128)} %bitcast.208) | data formatting | bytes 8388608
  42.0 5.2 all-to-all-start
  47.2 17.9 %fusion.9 = f32[1,2,4,32,32]{4,0,3,2,1:T(1,128)S(1)} fusion(f32[1,4,32,32,128]{4,3,2,1,0:T(8,128)} %copy-done.3, f32[1,4,32,32,128]{4,3,2,1,0:T(8,128)S(1)} %bitcast.224), kind=kOutput, calls=%fused_computation.25 | convolution fusion | flops 13632640 | bytes 4227072 | tf_op jit(solution)/shard_map/fsxyz,z->fsxy/dot_general | solution.py:21
  65.2 36.4 %all_gather.3 = f32[2,4,32,128]{2,1,0,3:T(4,128)S(1)} all-gather(f32[2,4,32,32]{2,1,0,3:T(4,128)S(1)} %bitcast.230), channel_id=1, replica_groups=mesh['sp'=2,'py'=4,'pz'=4] {'pz'}, dimensions={3}, use_global_device_ids=true | all-gather | bytes 163840 | tf_op jit(solution)/shard_map/all_gather | solution.py:59
  102.4 16.1 %reduce = f32[4,262144]{1,0:T(4,128)} reduce(f32[4,1,262144]{2,1,0:T(1,128)} %all-to-all-done, f32[]{:T(128)} %broadcast.307), dimensions={1}, to_apply=%all_to_all.72.reduce_sub_computation | reduce | bytes 8388612 | tf_op jit(solution)/shard_map/all_to_all | solution.py:56
  118.5 13.7 %reshape.176 = f32[64,2,2,4,32,32]{5,4,3,2,1,0:T(8,128)} reshape(f32[4,262144]{1,0:T(4,128)} %reduce) | data formatting | bytes 8388608
  132.2 21.0 %copy.171 = f32[2,2,4,32,4,32,16]{5,4,3,6,2,1,0:T(4,128)} copy(f32[2,2,4,32,4,32,16]{5,3,2,1,0,6,4:T(8,128)} %bitcast.209) | data formatting | bytes 8388608 | tf_op jit(solution)/shard_map/all_to_all | solution.py:56
  153.2 13.6 %all_to_all.75 = f32[2,2,4,32,128,16]{4,3,5,2,1,0:T(8,128)} reshape(f32[2,2,4,32,4,32,16]{5,4,3,6,2,1,0:T(4,128)} %copy.171) | data formatting | bytes 8388608 | tf_op jit(solution)/shard_map/all_to_all | solution.py:56
  166.9 3.9 fusion.32
  170.8 2.1 fusion.28
  172.9 2.3 add_bitcast_fusion.1
  175.2 2.3 subtract_bitcast_fusion.1
  177.5 2.9 pad_maximum_fusion.1
  180.4 15.2 %copy.177 = f32[2,2,4,32,128,17]{3,2,5,1,0,4:T(4,128)} copy(f32[2,2,4,32,128,17]{4,3,5,2,1,0:T(8,128)} %pad_maximum_fusion.1) | data formatting | bytes 8912896 | tf_op jit(solution)/shard_map/stack | solution.py:32
  195.6 22.2 %reshape.177 = f32[2,1,557056]{2,1,0:T(1,128)} reshape(f32[128,2,2,17,4,32]{5,4,3,2,1,0:T(4,128)} %bitcast.204) | data formatting | bytes 8912896
  217.8 12.4 %all_to_all.99 = f32[2,1,557056]{2,1,0:T(1,128)} all-to-all(f32[2,1,557056]{2,1,0:T(1,128)} %reshape.177), channel_id=1, replica_groups=mesh['sp'=2,'py'=4,'pz'=4] {'sp'}, dimensions={0} | all-to-all | bytes 8912896 | tf_op jit(solution)/shard_map/all_to_all | solution.py:70
  230.2 17.5 %reduce.1 = f32[2,557056]{1,0:T(2,128)} reduce(f32[2,1,557056]{2,1,0:T(1,128)} %all_to_all.99, f32[]{:T(128)} %broadcast.307), dimensions={1}, to_apply=%all_to_all.76.reduce_sub_computation | reduce | bytes 8912900 | tf_op jit(solution)/shard_map/all_to_all | solution.py:70
  247.7 23.0 %reshape.178 = f32[128,2,2,17,4,32]{5,4,3,2,1,0:T(4,128)} reshape(f32[2,557056]{1,0:T(2,128)} %reduce.1) | data formatting | bytes 8912896
  270.7 20.5 %copy.258 = f32[2,2,4,32,2,64,17]{5,4,3,6,2,1,0:T(2,128)} copy(f32[2,2,4,32,2,64,17]{3,2,6,1,0,5,4:T(4,128)} %bitcast.205) | data formatting | bytes 8912896 | tf_op jit(solution)/shard_map/all_to_all | solution.py:70
  291.2 8.3 %copy.179 = f32[2,2,2,4,32,64,17]{5,4,6,3,2,1,0:T(8,128)} copy(f32[2,2,2,4,32,64,17]{5,2,4,6,3,1,0:T(2,128)} %bitcast.215) | data formatting | bytes 8912896 | tf_op jit(solution)/shard_map/all_to_all | solution.py:70
  299.5 17.6 %copy.180 = f32[2,2,8,32,64,17]{3,2,5,1,0,4:T(8,128)} copy(f32[2,2,8,32,64,17]{4,3,5,2,1,0:T(8,128)} %bitcast.216) | data formatting | bytes 8912896 | tf_op jit(solution)/shard_map/all_to_all | solution.py:70
  317.0 21.0 %reshape.179 = f32[4,1,278528]{2,1,0:T(1,128)} reshape(f32[64,2,2,17,8,32]{5,4,3,2,1,0:T(8,128)} %bitcast.206) | data formatting | bytes 8912896
  338.0 5.1 all-to-all-start.2
  346.1 96.4 %all-to-all-done.2 = f32[4,1,278528]{2,1,0:T(1,128)} async-done(((f32[4,1,278528]{2,1,0:T(1,128)}), f32[4,1,278528]{2,1,0:T(1,128)}, u32[]{:S(2)}, u32[]{:S(2)}) %all-to-all-start.2) | async-done | bytes 4456480 | tf_op jit(solution)/shard_map/all_to_all | solution.py:69
  442.5 16.0 %reduce.2 = f32[4,278528]{1,0:T(4,128)} reduce(f32[4,1,278528]{2,1,0:T(1,128)} %all-to-all-done.2, f32[]{:T(128)} %broadcast.307), dimensions={1}, to_apply=%all_to_all.80.reduce_sub_computation | reduce | bytes 8912900 | tf_op jit(solution)/shard_map/all_to_all | solution.py:69
  458.5 14.6 %reshape.180 = f32[64,2,2,17,8,32]{5,4,3,2,1,0:T(8,128)} reshape(f32[4,278528]{1,0:T(4,128)} %reduce.2) | data formatting | bytes 8912896
  473.1 9.9 %copy.181 = f32[2,2,8,32,64,17]{3,4,5,2,1,0:T(8,128)S(1)} copy(f32[2,2,8,32,64,17]{3,2,5,1,0,4:T(8,128)} %bitcast.207) | data formatting | bytes 8912896 | tf_op jit(solution)/shard_map/all_to_all | solution.py:69
  483.0 7.4 fusion.166
  490.5 10.5 %copy.273 = f32[1,2,8,4,32,16,17]{4,3,6,5,2,1,0:T(4,128)} copy(f32[1,2,8,4,32,16,17]{4,5,3,6,2,1,0:T(8,128)} %get-tuple-element.5) | data formatting | bytes 4456448 | tf_op jit(solution)/shard_map/squeeze | solution.py:26
  501.0 7.4 reshape.173
  508.4 4.7 fusion.49
  513.0 10.4 %copy.274 = f32[1,2,8,4,32,16,17]{4,3,6,5,2,1,0:T(4,128)} copy(f32[1,2,8,4,32,16,17]{4,5,3,6,2,1,0:T(8,128)} %get-tuple-element.6) | data formatting | bytes 4456448 | tf_op jit(solution)/shard_map/squeeze | solution.py:26
  523.4 8.9 %reshape.174 = f32[2,8,128,16,17]{2,4,3,1,0:T(8,128)} reshape(f32[1,2,8,4,32,16,17]{4,3,6,5,2,1,0:T(4,128)} %copy.274) | data formatting | bytes 4456448 | tf_op jit(solution)/shard_map/squeeze | solution.py:26
  532.4 5.0 fusion.45
  537.4 3.1 add_bitcast_fusion
  540.5 3.1 subtract_bitcast_fusion
  544.1 3.6 fusion.15
  555.9 5.5 all_to_all.100
  561.7 6.7 copy.202
  568.4 7.7 reshape.181
  576.2 55.0 %all_to_all.101 = f32[4,1,139264]{2,1,0:T(1,128)} all-to-all(f32[4,1,139264]{2,1,0:T(1,128)S(1)} %reshape.181), channel_id=1, replica_groups=mesh['sp'=2,'py'=4,'pz'=4] {'py'}, dimensions={0} | all-to-all | bytes 4456448 | tf_op jit(solution)/shard_map/all_to_all | solution.py:90
  631.2 7.7 reduce.3
  639.0 8.3 %reshape.182 = f32[128,2,17,4,32]{4,3,2,1,0:T(4,128)} reshape(f32[4,139264]{1,0:T(4,128)S(1)} %reduce.3) | data formatting | bytes 4456448
  647.3 12.1 %copy.204 = f32[2,4,32,4,32,17]{2,4,5,3,1,0:T(8,128)} copy(f32[2,4,32,4,32,17]{4,1,5,0,2,3:T(4,128)} %bitcast.218) | data formatting | bytes 4456448 | tf_op jit(solution)/shard_map/all_to_all | solution.py:90
  659.4 4.7 fusion.167
  664.8 7.1 fusion.55
  672.5 7.3 fusion.51
  679.8 7.1 fusion.27
  687.0 7.1 fusion.26
  694.3 7.9 %copy.215 = f32[2,4,32,128,16]{2,4,1,0,3:T(8,128)} copy(f32[2,4,32,128,16]{3,2,4,1,0:T(8,128)S(1)} %pad_maximum_fusion.13) | data formatting | bytes 4194304 | tf_op jit(solution)/shard_map/slice | solution.py:100
  702.2 7.1 reshape.183
  709.3 4.5 all-to-all-start.5
  713.9 24.5 %all-to-all-done.5 = f32[4,1,131072]{2,1,0:T(1,128)} async-done(((f32[4,1,131072]{2,1,0:T(1,128)}), f32[4,1,131072]{2,1,0:T(1,128)}, u32[]{:S(2)}, u32[]{:S(2)}) %all-to-all-start.5) | async-done | bytes 2097184 | tf_op jit(solution)/shard_map/all_to_all | solution.py:102
  738.4 7.6 reduce.4
  746.1 6.1 reshape.184
  752.2 11.8 %copy.216 = f32[2,4,32,4,32,16]{4,5,3,2,1,0:T(8,128)} copy(f32[2,4,32,4,32,16]{2,5,1,0,4,3:T(8,128)} %bitcast.220) | data formatting | bytes 4194304 | tf_op jit(solution)/shard_map/all_to_all | solution.py:102
  764.0 4.4 fusion.168
  768.4 6.8 fusion
  775.2 8.6 %add_multiply_fusion = f32[4,32,32,128]{3,2,1,0:T(8,128)} fusion(f32[4,32,32,128]{3,2,1,0:T(8,128)S(1)} %fusion, f32[4,32,32,64]{2,3,1,0:T(8,128)S(1)} %bitcast.225, f32[64]{0:T(128)S(1)} %compare_select_fusion.3, f32[128]{0:T(128)S(1)} %fusion.81, f32[4,32,32]{2,1,0:T(8,128)S(1)} %dynamic-slice_bitcast_fusion, f32[128,128]{0,1:T(8,128)S(1)} %copy-done.9), kind=kOutput, calls=%fused_computation.40 | convolution fusion | flops 405012480 | bytes 5325568 | tf_op jit(solution)/shard_map/sxyk,kz->sxyz/dot_general | solution.py:21
  (59 shorter events, 15.0 us)
Async XLA Ops:
  0.0 343.1 %copy-start = (f32[8,8]{1,0:T(8,128)S(1)}, f32[8,8]{1,0:T(8,128)}, u32[]{:S(2)}) copy-start(f32[8,8]{1,0:T(8,128)} %param.5) | copy-start | bytes 772
  0.0 2.7 copy-start.2
  0.3 2.5 copy-start.8
  0.5 5.6 copy-start.10
  2.7 3.5 copy-start.3
  42.0 59.9 %all-to-all-start = ((f32[4,1,262144]{2,1,0:T(1,128)}), f32[4,1,262144]{2,1,0:T(1,128)}, u32[]{:S(2)}, u32[]{:S(2)}) async-start(f32[4,1,262144]{2,1,0:T(1,128)} %reshape.175), calls=%async_computation | async-start | bytes 8388608 | tf_op jit(solution)/shard_map/all_to_all | solution.py:56
  166.9 3.9 copy-start.1
  338.0 5.9 copy-start.12
  338.0 104.5 %all-to-all-start.2 = ((f32[4,1,278528]{2,1,0:T(1,128)}), f32[4,1,278528]{2,1,0:T(1,128)}, u32[]{:S(2)}, u32[]{:S(2)}) async-start(f32[4,1,278528]{2,1,0:T(1,128)} %reshape.179), calls=%async_computation.2 | async-start | bytes 8912896 | tf_op jit(solution)/shard_map/all_to_all | solution.py:69
  532.4 5.0 copy-start.4
  532.4 5.0 copy-start.5
  540.5 3.1 copy-start.7
  544.1 3.6 copy-start.6
  709.3 29.1 %all-to-all-start.5 = ((f32[4,1,131072]{2,1,0:T(1,128)}), f32[4,1,131072]{2,1,0:T(1,128)}, u32[]{:S(2)}, u32[]{:S(2)}) async-start(f32[4,1,131072]{2,1,0:T(1,128)} %reshape.183), calls=%async_computation.5 | async-start | bytes 4194304 | tf_op jit(solution)/shard_map/all_to_all | solution.py:102
  764.0 4.4 copy-start.11
  768.3 6.8 copy-start.9
where the time goes:
time: 795 us; the launch traced here: 784 us
  local copies, waits for them, and re-layouts  354 us (45%)
  waiting for transfers between devices  121 us (15%)
  blocking collectives  109 us (14%)
  matrix products  105 us (13%)
  other arithmetic  78.8 us (10%)
  starting transfers between devices  14.7 us (2%)
    unnamed x36, local copies, waits for them, and re-layouts  135 us
    dot_general x21, matrix products, contract(): return jnp.einsum(form, values, table, precision=lax.Precision.HIGHEST)  102 us
    all_to_all x1, waiting for transfers between devices, per_device(): lax.all_to_all(lax.all_to_all(spectrum, 'sp', split_axis=4, concat_axis=2...  96.4 us
    all_to_all x1, blocking collectives, per_device(): lax.all_to_all(lax.all_to_all(new_hat, 'sp', split_axis=1, concat_axis=3,...  55 us
    all_to_all x3, local copies, waits for them, and re-layouts, per_device(): lax.all_to_all(spectrum, 'sp', split_axis=4, concat_axis=2, tiled=True)  46.4 us
    squeeze x4, local copies, waits for them, and re-layouts, rotate(): real_part, imag_part = (spectrum[0], spectrum[1])  37.2 us
    all_gather x1, blocking collectives, per_device(): highest = lax.all_gather(highest, 'pz', axis=3, tiled=True)  36.4 us
    all_to_all x3, local copies, waits for them, and re-layouts, per_device(): lax.all_to_all(spectrum, 'pz', split_axis=5, concat_axis=4, tiled=True)  35.2 us
  transfers between devices with their start and end apart: 3, of which 2 were waited for; matrix products, arithmetic and copies ran while one was open for 3% of the time, Pallas kernels for 0%

commit v1 on v0

--- a/solution.py
+++ b/solution.py
@@ -66,13 +66,19 @@
         ]
     )
     spectrum = rotate(spectrum, "fsxyz,yk->fsxkz", full_y, True)
-    spectrum = lax.all_to_all(
-        lax.all_to_all(spectrum, "sp", split_axis=4, concat_axis=2, tiled=True),
-        "py",
-        split_axis=4,
-        concat_axis=3,
-        tiled=True,
-    )
+    x = lax.all_to_all(spectrum, "sp", split_axis=4, concat_axis=2, tiled=True)
+    ways, here = (lax.axis_size("py"), lax.axis_index("py"))
+    width = x.shape[4] // ways
+    shape = list(x.shape)
+    shape[4] = width
+    height = shape[3]
+    shape[3] = height * ways
+    spectrum = jnp.zeros(shape, x.dtype)
+    for mask in range(ways):
+        part = lax.dynamic_slice_in_dim(x, (here ^ mask) * width, width, axis=4)
+        if mask:
+            part = lax.ppermute(part, "py", [(d, d ^ mask) for d in range(ways)])
+        spectrum = lax.dynamic_update_slice_in_dim(spectrum, part, (here ^ mask) * height, axis=3)
     spectrum = rotate(spectrum, "fsxyz,xk->fskyz", full_x, True)
     narrow = spectrum.shape[4]
     lines = spectrum.shape[5]

time: 795 us -> 1060 us (1.33)
  local copies, waits for them, and re-layouts: 354 us -> 568 us
  waiting for transfers between devices: 121 us -> 187 us
  other arithmetic: 78.8 us -> 62 us
    dynamic_update_slice x0 -> x4, local copies, waits for them, and re-layouts: none -> 283 us  [per_device(): lax.dynamic_update_slice_in_dim(spectrum, part, (here ^ mask) * height, a...]
    ppermute x0 -> x3, waiting for transfers between devices: none -> 163 us  [per_device(): part = lax.ppermute(part, 'py', [(d, d ^ mask) for d in range(ways)])]
    all_to_all x1 -> x0, waiting for transfers between devices: 96.4 us -> none  [per_device(): lax.all_to_all(lax.all_to_all(spectrum, 'sp', split_axis=4, concat_axis=2...]
    all_to_all x4 -> x1, local copies, waits for them, and re-layouts: 56.3 us -> 16 us  [per_device(): x = lax.all_to_all(spectrum, 'sp', split_axis=4, concat_axis=2, tiled=True)]
    squeeze x4 -> x0, local copies, waits for them, and re-layouts: 37.2 us -> none  [rotate(): real_part, imag_part = (spectrum[0], spectrum[1])]
    unnamed x36 -> x30, local copies, waits for them, and re-layouts: 135 us -> 99.7 us
    dynamic_slice x0 -> x4, local copies, waits for them, and re-layouts: none -> 27 us  [per_device(): part = lax.dynamic_slice_in_dim(x, (here ^ mask) * width, width, axis=4)]
    ppermute x0 -> x3, local copies, waits for them, and re-layouts: none -> 20.8 us  [per_device(): part = lax.ppermute(part, 'py', [(d, d ^ mask) for d in range(ways)])]
  transfers between devices with their start and end apart: 3 -> 5, of which waited for: 2 -> 3; matrix products, arithmetic and copies ran while one was open for 3% -> 23% of each run, Pallas kernels for 0% -> 0%
where the time goes in v1:
time: 1060 us; the launch traced here: 1050 us
  local copies, waits for them, and re-layouts  568 us (54%)
  waiting for transfers between devices  187 us (18%)
  blocking collectives  110 us (10%)
  matrix products  104 us (10%)
  other arithmetic  62 us (6%)
  starting transfers between devices  14 us (1%)
    dynamic_update_slice x4, local copies, waits for them, and re-layouts, per_device(): lax.dynamic_update_slice_in_dim(spectrum, part, (here ^ mask) * height, a...  283 us
    ppermute x3, waiting for transfers between devices, per_device(): part = lax.ppermute(part, 'py', [(d, d ^ mask) for d in range(ways)])  163 us
    dot_general x21, matrix products, contract(): return jnp.einsum(form, values, table, precision=lax.Precision.HIGHEST)  100 us
    unnamed x30, local copies, waits for them, and re-layouts  99.7 us
    all_to_all x1, blocking collectives, per_device(): lax.all_to_all(lax.all_to_all(new_hat, 'sp', split_axis=1, concat_axis=3,...  55.6 us
    all_gather x1, blocking collectives, per_device(): highest = lax.all_gather(highest, 'pz', axis=3, tiled=True)  36.4 us
    all_to_all x3, local copies, waits for them, and re-layouts, per_device(): lax.all_to_all(spectrum, 'pz', split_axis=5, concat_axis=4, tiled=True)  35.3 us
    dynamic_slice x4, local copies, waits for them, and re-layouts, per_device(): part = lax.dynamic_slice_in_dim(x, (here ^ mask) * width, width, axis=4)  27 us
  transfers between devices with their start and end apart: 5, of which 3 were waited for; matrix products, arithmetic and copies ran while one was open for 23% of the time, Pallas kernels for 0%

profile of v1, /device:TPU:0, one launch (start us, length us, event | category | flops | bytes accessed | tf_op | source)
XLA Modules:
  0.0 1045.5 jit_solution(12177820973575505600)
XLA Ops:
  2.7 3.4 fusion.21
  6.2 3.4 negate_bitcast_fusion
  9.6 4.3 pad_maximum_fusion
  13.9 16.6 %copy.159 = f32[2,2,4,32,32,64]{4,3,2,1,0,5:T(8,128)} copy(f32[2,2,4,32,32,64]{5,4,3,2,1,0:T(8,128)} %pad_maximum_fusion) | data formatting | bytes 8388608 | tf_op jit(solution)/shard_map/stack | solution.py:50
  30.5 11.5 %reshape.169 = f32[4,1,262144]{2,1,0:T(1,128)} reshape(f32[64,2,2,4,32,32]{5,4,3,2,1,0:T(8,128)} %bitcast.206) | data formatting | bytes 8388608
  41.9 5.2 all-to-all-start
  47.1 17.9 %fusion.13 = f32[1,2,4,32,32]{4,0,3,2,1:T(1,128)S(1)} fusion(f32[1,4,32,32,128]{4,3,2,1,0:T(8,128)} %copy-done.4, f32[1,4,32,32,128]{4,3,2,1,0:T(8,128)S(1)} %bitcast.220), kind=kOutput, calls=%fused_computation.31 | convolution fusion | flops 13632640 | bytes 4227072 | tf_op jit(solution)/shard_map/fsxyz,z->fsxy/dot_general | solution.py:21
  65.1 36.4 %all_gather.3 = f32[2,4,32,128]{2,1,0,3:T(4,128)S(1)} all-gather(f32[2,4,32,32]{2,1,0,3:T(4,128)S(1)} %bitcast.226), channel_id=1, replica_groups=mesh['sp'=2,'py'=4,'pz'=4] {'pz'}, dimensions={3}, use_global_device_ids=true | all-gather | bytes 163840 | tf_op jit(solution)/shard_map/all_gather | solution.py:59
  102.5 16.2 %reduce = f32[4,262144]{1,0:T(4,128)} reduce(f32[4,1,262144]{2,1,0:T(1,128)} %all-to-all-done, f32[]{:T(128)} %broadcast.307), dimensions={1}, to_apply=%all_to_all.61.reduce_sub_computation | reduce | bytes 8388612 | tf_op jit(solution)/shard_map/all_to_all | solution.py:56
  118.7 13.7 %reshape.170 = f32[64,2,2,4,32,32]{5,4,3,2,1,0:T(8,128)} reshape(f32[4,262144]{1,0:T(4,128)} %reduce) | data formatting | bytes 8388608
  132.5 21.0 %copy.161 = f32[2,2,4,32,4,32,16]{5,4,3,6,2,1,0:T(4,128)} copy(f32[2,2,4,32,4,32,16]{5,3,2,1,0,6,4:T(8,128)} %bitcast.207) | data formatting | bytes 8388608 | tf_op jit(solution)/shard_map/all_to_all | solution.py:56
  153.5 13.7 %all_to_all.64 = f32[2,2,4,32,128,16]{4,3,5,2,1,0:T(8,128)} reshape(f32[2,2,4,32,4,32,16]{5,4,3,6,2,1,0:T(4,128)} %copy.161) | data formatting | bytes 8388608 | tf_op jit(solution)/shard_map/all_to_all | solution.py:56
  167.1 3.9 fusion.36
  173.2 2.3 add_bitcast_fusion.1
  175.5 2.3 subtract_bitcast_fusion.1
  177.8 2.9 pad_maximum_fusion.1
  180.6 15.3 %copy.167 = f32[2,2,4,32,128,17]{3,2,5,1,0,4:T(4,128)} copy(f32[2,2,4,32,128,17]{4,3,5,2,1,0:T(8,128)} %pad_maximum_fusion.1) | data formatting | bytes 8912896 | tf_op jit(solution)/shard_map/stack | solution.py:32
  195.9 22.3 %reshape.171 = f32[2,1,557056]{2,1,0:T(1,128)} reshape(f32[128,2,2,17,4,32]{5,4,3,2,1,0:T(4,128)} %bitcast.204) | data formatting | bytes 8912896
  218.2 12.4 %all_to_all.84 = f32[2,1,557056]{2,1,0:T(1,128)} all-to-all(f32[2,1,557056]{2,1,0:T(1,128)} %reshape.171), channel_id=1, replica_groups=mesh['sp'=2,'py'=4,'pz'=4] {'sp'}, dimensions={0} | all-to-all | bytes 8912896 | tf_op jit(solution)/shard_map/all_to_all | solution.py:69
  230.6 17.6 %reduce.1 = f32[2,557056]{1,0:T(2,128)} reduce(f32[2,1,557056]{2,1,0:T(1,128)} %all_to_all.84, f32[]{:T(128)} %broadcast.307), dimensions={1}, to_apply=%all_to_all.65.reduce_sub_computation | reduce | bytes 8912900 | tf_op jit(solution)/shard_map/all_to_all | solution.py:69
  248.2 22.9 %reshape.172 = f32[128,2,2,17,4,32]{5,4,3,2,1,0:T(4,128)} reshape(f32[2,557056]{1,0:T(2,128)} %reduce.1) | data formatting | bytes 8912896
  271.2 16.0 %copy.168 = f32[2,2,4,32,2,64,17]{3,6,5,2,4,1,0:T(8,128)} copy(f32[2,2,4,32,2,64,17]{3,2,6,1,0,5,4:T(4,128)} %bitcast.205) | data formatting | bytes 8912896 | tf_op jit(solution)/shard_map/all_to_all | solution.py:69
  287.2 15.5 %constant_dynamic-slice_fusion = (f32[2,2,8,32,16,17]{3,5,4,2,1,0:T(8,128)S(1)}, f32[2,2,8,32,16,17]{3,5,4,2,1,0:T(8,128)}, f32[2,2,8,32,16,17]{3,5,4,2,1,0:T(8,128)}, f32[2,2,8,32,16,17]{3,5,4,2,1,0:T(8,128)}) fusion(f32[2,2,8,32,64,17]{3,5,4,2,1,0:T(8,128)} %bitcast.203, s32[]{:T(128)S(6)} %select_n.138, s32[]{:T(128)S(6)} %select_n.136, ...), kind=kLoop, calls=%fused_computation.124 | loop fusion | bytes 8912912 | tf_op jit(solution)/shard_map/dynamic_slice | solution.py:78
  302.7 5.8 copy.169
  310.1 2.9 copy.171
  312.9 2.6 collective-permute-start.1
  315.5 2.8 copy.173
  319.8 3.4 broadcast_in_dim.12
  323.2 25.6 %dynamic_update_slice.12 = f32[2,2,8,128,16,17]{3,5,4,2,1,0:T(8,128)} dynamic-update-slice(f32[2,2,8,128,16,17]{3,5,4,2,1,0:T(8,128)} %broadcast_in_dim.12, f32[2,2,8,32,16,17]{3,5,4,2,1,0:T(8,128)} %get-tuple-element.8, s32[]{:T(128)} %constant.103.clone.1, s32[]{:T(128)} %constant.103.clone.1, s32[]{:T(128)} %constant.103.clone.1, s32[]{:T(128)S(6)} %select_n.133, s32[]{:T(128)} %constant.103.clone.1, ...) | dynamic-update-slice | bytes 2228228 | tf_op jit(solution)/shard_map/dynamic_update_slice | solution.py:81
  348.8 150.7 %collective-permute-done = f32[2,2,8,32,16,17]{3,4,5,2,1,0:T(8,128)} collective-permute-done((f32[2,2,8,32,16,17]{3,4,5,2,1,0:T(8,128)}, f32[2,2,8,32,16,17]{3,4,5,2,1,0:T(8,128)}, u32[]{:S(2)}, u32[]{:S(2)}) %collective-permute-start) | collective-permute-done | bytes 1114144 | tf_op jit(solution)/shard_map/ppermute | solution.py:80
  499.5 6.9 copy.170
  506.4 85.9 %dynamic_update_slice.13 = f32[2,2,8,128,16,17]{3,5,4,2,1,0:T(8,128)} dynamic-update-slice(f32[2,2,8,128,16,17]{3,5,4,2,1,0:T(8,128)} %dynamic_update_slice.12, f32[2,2,8,32,16,17]{3,5,4,2,1,0:T(8,128)} %copy.170, s32[]{:T(128)} %constant.103.clone.1, s32[]{:T(128)} %constant.103.clone.1, s32[]{:T(128)} %constant.103.clone.1, s32[]{:T(128)S(6)} %select_n.135, s32[]{:T(128)} %constant.103.clone.1, ...) | dynamic-update-slice | bytes 2228228 | tf_op jit(solution)/shard_map/dynamic_update_slice | solution.py:81
  592.4 11.9 %collective-permute-done.1 = f32[2,2,8,32,16,17]{3,4,5,2,1,0:T(8,128)} collective-permute-done((f32[2,2,8,32,16,17]{3,4,5,2,1,0:T(8,128)}, f32[2,2,8,32,16,17]{3,4,5,2,1,0:T(8,128)}, u32[]{:S(2)}, u32[]{:S(2)}) %collective-permute-start.1) | collective-permute-done | bytes 1114144 | tf_op jit(solution)/shard_map/ppermute | solution.py:80
  604.2 6.9 copy.172
  611.1 85.9 %dynamic_update_slice.14 = f32[2,2,8,128,16,17]{3,5,4,2,1,0:T(8,128)} dynamic-update-slice(f32[2,2,8,128,16,17]{3,5,4,2,1,0:T(8,128)} %dynamic_update_slice.13, f32[2,2,8,32,16,17]{3,5,4,2,1,0:T(8,128)} %copy.172, s32[]{:T(128)} %constant.103.clone.1, s32[]{:T(128)} %constant.103.clone.1, s32[]{:T(128)} %constant.103.clone.1, s32[]{:T(128)S(6)} %select_n.137, s32[]{:T(128)} %constant.103.clone.1, ...) | dynamic-update-slice | bytes 2228228 | tf_op jit(solution)/shard_map/dynamic_update_slice | solution.py:81
  697.1 6.9 copy.174
  704.0 86.1 %dynamic_update_slice.15 = f32[2,2,8,128,16,17]{3,5,4,2,1,0:T(8,128)} dynamic-update-slice(f32[2,2,8,128,16,17]{3,5,4,2,1,0:T(8,128)} %dynamic_update_slice.14, f32[2,2,8,32,16,17]{3,5,4,2,1,0:T(8,128)} %copy.174, s32[]{:T(128)} %constant.103.clone.1, s32[]{:T(128)} %constant.103.clone.1, s32[]{:T(128)} %constant.103.clone.1, s32[]{:T(128)S(6)} %select_n.139, s32[]{:T(128)} %constant.103.clone.1, ...) | dynamic-update-slice | bytes 2228228 | tf_op jit(solution)/shard_map/dynamic_update_slice | solution.py:81
  790.1 5.0 fusion.12
  795.1 3.0 fusion.9
  798.1 3.1 add_bitcast_fusion
  801.2 3.1 subtract_bitcast_fusion
  804.9 3.4 fusion.19
  817.0 5.5 all_to_all.85
  822.8 6.7 copy.189
  829.5 7.7 reshape.173
  837.2 55.6 %all_to_all.86 = f32[4,1,139264]{2,1,0:T(1,128)} all-to-all(f32[4,1,139264]{2,1,0:T(1,128)S(1)} %reshape.173), channel_id=1, replica_groups=mesh['sp'=2,'py'=4,'pz'=4] {'py'}, dimensions={0} | all-to-all | bytes 4456448 | tf_op jit(solution)/shard_map/all_to_all | solution.py:96
  892.9 7.9 reduce.2
  900.7 8.3 reshape.174
  909.0 11.9 %copy.191 = f32[2,4,32,4,32,17]{2,4,5,3,1,0:T(8,128)} copy(f32[2,4,32,4,32,17]{4,1,5,0,2,3:T(4,128)} %bitcast.214) | data formatting | bytes 4456448 | tf_op jit(solution)/shard_map/all_to_all | solution.py:96
  920.9 4.7 fusion.168
  926.3 7.1 fusion.57
  934.1 7.3 fusion.53
  941.4 7.1 fusion.31
  948.5 7.1 fusion.30
  955.9 8.0 copy.202
  963.9 7.1 reshape.175
  971.0 4.4 all-to-all-start.4
  975.5 24.4 %all-to-all-done.4 = f32[4,1,131072]{2,1,0:T(1,128)} async-done(((f32[4,1,131072]{2,1,0:T(1,128)}), f32[4,1,131072]{2,1,0:T(1,128)}, u32[]{:S(2)}, u32[]{:S(2)}) %all-to-all-start.4) | async-done | bytes 2097184 | tf_op jit(solution)/shard_map/all_to_all | solution.py:108
  999.9 7.8 reduce.3
  1007.7 6.1 reshape.176
  1013.8 11.7 %copy.203 = f32[2,4,32,4,32,16]{4,5,3,2,1,0:T(8,128)} copy(f32[2,4,32,4,32,16]{2,5,1,0,4,3:T(8,128)} %bitcast.216) | data formatting | bytes 4194304 | tf_op jit(solution)/shard_map/all_to_all | solution.py:108
  1025.5 4.4 fusion.169
  1029.9 6.8 fusion
  1036.8 8.6 add_multiply_fusion
  (60 shorter events, 20.1 us)
Async XLA Ops:
  0.0 318.5 %copy-start = (f32[8,8]{1,0:T(8,128)S(1)}, f32[8,8]{1,0:T(8,128)}, u32[]{:S(2)}) copy-start(f32[8,8]{1,0:T(8,128)} %param.5) | copy-start | bytes 772
  0.0 2.7 copy-start.3
  0.3 2.5 copy-start.6
  0.5 5.6 copy-start.8
  2.7 3.5 copy-start.4
  41.9 60.0 %all-to-all-start = ((f32[4,1,262144]{2,1,0:T(1,128)}), f32[4,1,262144]{2,1,0:T(1,128)}, u32[]{:S(2)}, u32[]{:S(2)}) async-start(f32[4,1,262144]{2,1,0:T(1,128)} %reshape.169), calls=%async_computation | async-start | bytes 8388608 | tf_op jit(solution)/shard_map/all_to_all | solution.py:56
  167.1 3.9 copy-start.1
  302.7 7.4 copy-start.5
  308.4 191.1 %collective-permute-start = (f32[2,2,8,32,16,17]{3,4,5,2,1,0:T(8,128)}, f32[2,2,8,32,16,17]{3,4,5,2,1,0:T(8,128)}, u32[]{:S(2)}, u32[]{:S(2)}) collective-permute-start(f32[2,2,8,32,16,17]{3,4,5,2,1,0:T(8,128)} %copy.169), channel_id=1, source_target_pairs={{0,4},{4,0},{8,12},{12,8},{1,5},{5,1},{9,13},{13,9},{2,6},{6,2},{1... | collective-permute-start | bytes 3342344 | tf_op jit(solution)/shard_map/ppermute | solution.py:80
  312.9 291.3 %collective-permute-start.1 = (f32[2,2,8,32,16,17]{3,4,5,2,1,0:T(8,128)}, f32[2,2,8,32,16,17]{3,4,5,2,1,0:T(8,128)}, u32[]{:S(2)}, u32[]{:S(2)}) collective-permute-start(f32[2,2,8,32,16,17]{3,4,5,2,1,0:T(8,128)} %copy.171), channel_id=1, source_target_pairs={{0,8},{4,12},{8,0},{12,4},{1,9},{5,13},{9,1},{13,5},{2,10},{6,14},... | collective-permute-start | bytes 3342344 | tf_op jit(solution)/shard_map/ppermute | solution.py:80
  315.5 3.7 copy-start.10
  318.4 378.7 %collective-permute-start.2 = (f32[2,2,8,32,16,17]{3,4,5,2,1,0:T(8,128)}, f32[2,2,8,32,16,17]{3,4,5,2,1,0:T(8,128)}, u32[]{:S(2)}, u32[]{:S(2)}) collective-permute-start(f32[2,2,8,32,16,17]{3,4,5,2,1,0:T(8,128)} %copy.173), channel_id=1, source_target_pairs={{0,12},{4,8},{8,4},{12,0},{1,13},{5,9},{9,5},{13,1},{2,14},{6,10},... | collective-permute-start | bytes 3342344 | tf_op jit(solution)/shard_map/ppermute | solution.py:80
  790.1 5.0 copy-start.2
  971.0 28.9 %all-to-all-start.4 = ((f32[4,1,131072]{2,1,0:T(1,128)}), f32[4,1,131072]{2,1,0:T(1,128)}, u32[]{:S(2)}, u32[]{:S(2)}) async-start(f32[4,1,131072]{2,1,0:T(1,128)} %reshape.175), calls=%async_computation.4 | async-start | bytes 4194304 | tf_op jit(solution)/shard_map/all_to_all | solution.py:108
  1025.5 4.4 copy-start.9
  1029.9 6.8 copy-start.7
